TPU v7x, 32 devices: a whole 2x2x4 slice. The times are simulated.
32 devices in a mesh: kpt: 4 (over y, x), grid: 8 (over z, core).
Axes of the slice: x: 2, y: 2, z: 4, core: 2. Of those that a mesh axis runs over, the one named last changes fastest.
Arguments:
- bands: float32 [4, 2, 2, 48, 2304], P('kpt', None, None, 'grid'), may hold values from -6 to 6
- potential: float32 [48, 2304], P('grid'), may hold values from -4 to 4
- phase_numerator_table: int32 [4, 3], P('kpt'), may hold values from 0 to 7
- kweight: float32 [4], P('kpt'), may hold values from 0.25 to 2
- lowest: float32 [4], P('kpt'), may hold values from -6 to -4.5
- cut: float32 [4], P('kpt'), may hold values from 0 to 3
- upper: float32 [4], P('kpt'), may hold values from 15 to 17
- fermi: float32 [1], replicated, may hold values from -0.5 to 1.5
Outputs:
- filtered: float32 [4, 2, 2, 48, 2304], P('kpt', None, None, 'grid')
- band_energies: float32 [4, 2], P('kpt')
- total_energy: float32 [1], replicated
All inputs are finite; a program needn't handle non-finite values.
Results may differ from a plain program's by a relative error of at most 0.00022.
Values sent between devices are 32-bit elements; how exact they have to be, the bound alone decides.
A program may use at most 128 MiB of HBM per device.

v0:
```python
import functools

import jax
import jax.numpy as jnp
import numpy as np
from jax import lax
from jax.experimental import pallas as pl
from jax.experimental.pallas import tpu as pltpu
from jax.sharding import PartitionSpec as P

SIDE = 48
DEGREE = 6
PHASE_DIVISOR = 8
REACH = 6
LANES = 128
USED = 2 * SIDE
PAD = 8
ROWS = SIDE + 2 * PAD
HALF = SIDE // 2
TILES = SIDE // 8

coefficients = (
    -5369.0 / 1800.0,
    12.0 / 7.0,
    -15.0 / 56.0,
    10.0 / 189.0,
    -1.0 / 112.0,
    2.0 / 1925.0,
    -1.0 / 16632.0,
)
smearing = 0.5
MESH = pl.DeviceIdType.MESH


def third_parts():
    inside = np.zeros((SIDE, SIDE))
    over = np.zeros((SIDE, SIDE))
    under = np.zeros((SIDE, SIDE))
    for z in range(SIDE):
        for j in range(1, REACH + 1):
            weight = -0.5 * coefficients[j]
            for target, sign in ((z + j, 1), (z - j, -1)):
                if 0 <= target < SIDE:
                    inside[target, z] += weight
                elif sign > 0:
                    over[target - SIDE, z] += weight
                else:
                    under[target + SIDE, z] += weight
    plain = np.zeros((LANES, LANES))
    cosine = np.zeros((LANES, LANES))
    sine = np.zeros((LANES, LANES))
    both, apart = over + under, over - under
    for c in range(2):
        s = slice(c * SIDE, (c + 1) * SIDE)
        plain[s, s] = inside
        cosine[s, s] = both
    re, im = slice(0, SIDE), slice(SIDE, USED)
    sine[im, re] = -apart
    sine[re, im] = apart
    return [a.astype(np.float32) for a in (plain, cosine, sine)]


def kernel(
    n,
    members_k,
    table_ref,
    kweight_ref,
    lowest_ref,
    cut_ref,
    upper_ref,
    fermi_ref,
    packed_ref,
    pot_ref,
    parts_ref,
    out_ref,
    energy_ref,
    total_ref,
    field_0,
    field_1,
    field_2,
    mat_ref,
    potential,
    gathered,
    gathered_pot,
    part,
    part_k,
    send,
    recv,
    send_pot,
    recv_pot,
    send_red,
    recv_red,
    send_k,
    recv_k,
    swap_sem,
):
    planes = REACH
    chips = n // 2
    blocks = n
    home = (blocks - 2) // 2
    me = lax.axis_index("grid")
    kpt = lax.axis_index("kpt")
    chip, core = me // 2, me % 2
    partner = chip * 2 + (1 - core)

    barrier = pltpu.get_barrier_semaphore()
    for d in range(1, n):
        pl.semaphore_signal(barrier, inc=1, device_id=(kpt, (me + d) % n), device_id_type=MESH)
    for d in range(1, members_k):
        pl.semaphore_signal(
            barrier, inc=1, device_id=((kpt + d) % members_k, me), device_id_type=MESH
        )
    pl.semaphore_wait(barrier, n - 1 + members_k - 1)

    def remote(src, dst, ssem, rsem, target):
        return pltpu.make_async_remote_copy(
            src_ref=src,
            dst_ref=dst,
            send_sem=ssem,
            recv_sem=rsem,
            device_id=(kpt, target),
            device_id_type=MESH,
        )

    has_up, has_down = chip < chips - 1, chip > 0

    def own(which, ssem, target):
        return remote(packed_ref.at[which], gathered.at[me], ssem, recv.at[me], target)

    def own_pot(ssem, target):
        return remote(pot_ref, gathered_pot.at[me], ssem, recv_pot.at[me], target)

    @pl.when(has_up)
    def _():
        own(core, send.at[0], me + 2).start()
        own(1 - core, send.at[1], partner + 2).start()
        own_pot(send_pot.at[0], me + 2).start()

    @pl.when(has_down)
    def _():
        own(core, send.at[2], me - 2).start()
        own(1 - core, send.at[3], partner - 2).start()
        own_pot(send_pot.at[1], me - 2).start()

    own(1 - core, send.at[4], partner).start()
    own_pot(send_pot.at[2], partner).start()

    lane = lax.broadcasted_iota(jnp.int32, (8, LANES), 1)
    first = lane < SIDE
    used = lane < USED
    zero = jnp.zeros((8, LANES), jnp.float32)

    def turn(v, cosine, sine):
        other = jnp.where(first, pltpu.roll(v, LANES - SIDE, 1), pltpu.roll(v, SIDE, 1))
        signed = jnp.where(used, jnp.where(first, -sine, sine), 0.0)
        return cosine * v + signed * other

    def spread(scalar):
        return jnp.full((8, LANES), scalar)

    def phase(d):
        numerator = spread(table_ref[0, d])
        cosine, sine = jnp.ones((8, LANES), jnp.float32), zero
        for i in range(1, PHASE_DIVISOR):
            here = numerator == i
            angle = 2.0 * np.pi * i / PHASE_DIVISOR
            cosine = jnp.where(here, float(np.cos(angle)), cosine)
            sine = jnp.where(here, float(np.sin(angle)), sine)
        return cosine, sine

    cos_x, sin_x = phase(0)
    cos_y, sin_y = phase(1)
    cos_z, sin_z = phase(2)
    low_end, cut_end, high_end = (spread(r[0]) for r in (lowest_ref, cut_ref, upper_ref))
    half_width = (high_end - cut_end) / 2.0
    centre = (high_end + cut_end) / 2.0
    first_sigma = half_width / (low_end - centre)
    sigma = first_sigma
    recurrence = [(first_sigma / half_width, None)]
    for degree in range(1, DEGREE):
        next_sigma = 1.0 / (2.0 / first_sigma - sigma)
        recurrence.append((2.0 * next_sigma / half_width, sigma * next_sigma))
        sigma = next_sigma

    for r in range(LANES // 16):
        rows = pl.ds(16 * r, 16)
        cosine = jnp.concatenate([cos_z, cos_z], axis=0)
        sine = jnp.concatenate([sin_z, sin_z], axis=0)
        entry = parts_ref[0, rows, :] + cosine * parts_ref[1, rows, :] + sine * parts_ref[2, rows, :]
        high = entry.astype(jnp.bfloat16)
        rest = (entry - high.astype(jnp.float32)).astype(jnp.bfloat16)
        lower = pl.ds(LANES + 16 * r, 16)
        mat_ref[rows, pl.ds(0, LANES)] = high
        mat_ref[rows, pl.ds(LANES, LANES)] = rest
        mat_ref[lower, pl.ds(0, LANES)] = high
        mat_ref[lower, pl.ds(LANES, LANES)] = jnp.zeros_like(high)

    fields = (field_0, field_1, field_2)

    def put(field, plane, t, v):
        field[plane, pl.ds(PAD + 8 * t, 8), :] = v
        if t == 0:
            field[plane, pl.ds(PAD + SIDE, 8), :] = turn(v, cos_y, sin_y)
        if t == TILES - 1:
            field[plane, pl.ds(0, 8), :] = turn(v, cos_y, -sin_y)

    def unpack(load, slab):
        place = lax.rem(slab - 2 * chip + home + blocks, blocks)
        absolute = 2 * chip - home + place
        wrapped_low = absolute < 0
        wrapped_high = absolute >= blocks
        base = planes + place * planes

        def emit(change):
            for hp in range(2 * planes):
                plane, half = hp // 2, hp % 2
                for r in range(HALF // 8):
                    if hp < 9:
                        v = jnp.where(used, load(hp, r), zero)
                    else:
                        g = hp - 9
                        v = zero
                        for q in range(3):
                            piece = pltpu.roll(load(3 * g + q, r), 32 + 32 * q, 1)
                            inside = (lane >= 32 * q) & (lane < 32 * q + 32)
                            v = jnp.where(inside, piece, v)
                    put(field_0, base + plane, half * (HALF // 8) + r, change(v))

        wrapped = wrapped_low | wrapped_high

        @pl.when(wrapped)
        def _():
            way = jnp.where(wrapped_low, -1.0, 1.0)
            emit(lambda v: turn(v, cos_x, way * sin_x))

        @pl.when(jnp.logical_not(wrapped))
        def _():
            emit(lambda v: v)

    def unpack_pot(load, slab):
        place = lax.rem(slab - 2 * chip + home + blocks, blocks)
        for pair in range(planes // 2):
            for t in range(TILES):
                v = load(pair, t) - 1.5 * coefficients[0]
                swap_up = pltpu.roll(v, SIDE, 1)
                swap_down = pltpu.roll(v, LANES - SIDE, 1)
                rows = pl.ds(8 * t, 8)
                potential[place * planes + 2 * pair, rows, :] = jnp.where(first, v, swap_up)
                potential[place * planes + 2 * pair + 1, rows, :] = jnp.where(first, swap_down, v)

    def own_load(hp, r):
        return packed_ref[core, hp, pl.ds(8 * r, 8), :]

    unpack(own_load, me)
    unpack_pot(lambda pair, t: pot_ref[pair, pl.ds(8 * t, 8), :], me)

    def unpack_slab(slab):
        unpack(lambda hp, r: gathered[slab, hp, pl.ds(8 * r, 8), :], slab)

    def unpack_pot_slab(slab):
        unpack_pot(lambda pair, t: gathered_pot[slab, pair, pl.ds(8 * t, 8), :], slab)

    def await_slab(slab):
        remote(gathered.at[slab], gathered.at[slab], send.at[0], recv.at[slab], partner).wait_recv()

    def await_pot(slab):
        remote(
            gathered_pot.at[slab], gathered_pot.at[slab], send_pot.at[0], recv_pot.at[slab], partner
        ).wait_recv()

    def relay(slab, target):
        return remote(
            gathered.at[slab], gathered.at[slab], send.at[5 + slab], recv.at[slab], target
        )

    def relay_pot(slab, target, side):
        return remote(
            gathered_pot.at[slab],
            gathered_pot.at[slab],
            send_pot.at[3 + 2 * slab + side],
            recv_pot.at[slab],
            target,
        )

    def arrive(source, onward, target):
        for p in range(2):
            slab = 2 * source + p
            await_slab(slab)

            @pl.when(onward)
            def _():
                relay(slab, target).start()

        same = 2 * source + core
        await_pot(same)

        @pl.when(onward)
        def _():
            relay_pot(same, target, 0).start()

        relay_pot(same, partner, 1).start()

    def process(source):
        def one(p, carry):
            slab = 2 * source + p
            unpack_slab(slab)
            return carry

        lax.fori_loop(0, 2, one, 0)
        unpack_pot_slab(2 * source + core)

    def gather_step(d, carry):
        low_there, high_there = chip - d >= 0, chip + d < chips

        @pl.when(low_there)
        def _():
            arrive(chip - d, has_up, me + 2)

        @pl.when(high_there)
        def _():
            arrive(chip + d, has_down, me - 2)

        @pl.when(low_there)
        def _():
            process(chip - d)

        @pl.when(high_there)
        def _():
            process(chip + d)

        return carry

    await_slab(partner)
    unpack_slab(partner)
    await_pot(partner)
    unpack_pot_slab(partner)
    lax.fori_loop(1, chips, gather_step, 0)

    def other_pot(source, carry):
        @pl.when(source != chip)
        def _():
            slab = 2 * source + (1 - core)
            await_pot(slab)
            unpack_pot_slab(slab)

        return carry

    lax.fori_loop(0, chips, other_pot, 0)

    def wrap_planes(field):
        def one(i, carry):
            tiles = [pl.ds(8 * t, 8) for t in range(ROWS // 8)]
            lows = [field[blocks * planes + i, rows, :] for rows in tiles]
            highs = [field[planes + i, rows, :] for rows in tiles]
            lows = [turn(v, cos_x, -sin_x) for v in lows]
            highs = [turn(v, cos_x, sin_x) for v in highs]
            for rows, low, high in zip(tiles, lows, highs):
                field[i, rows, :] = low
                field[planes + blocks * planes + i, rows, :] = high
            return carry

        lax.fori_loop(0, planes, one, 0)

    wrap_planes(field_0)
    weights = [-0.5 * c for c in coefficients]

    def apply(m, k):
        field = fields[(m - 1) % 3]
        base = k * planes
        middle = [field[base + planes + p, pl.ds(PAD, SIDE), :] for p in range(planes)]
        rows = jnp.concatenate(middle, axis=0)
        high = rows.astype(jnp.bfloat16)
        rest = (rows - high.astype(jnp.float32)).astype(jnp.bfloat16)
        both = jnp.concatenate([high, rest], axis=1)
        third = jnp.dot(both, mat_ref[...], preferred_element_type=jnp.float32)
        third = third[:, :LANES] + third[:, LANES:]
        for t in range(TILES):
            tile = pl.ds(PAD + 8 * t, 8)
            window = [field[base + i, tile, :] for i in range(3 * planes)]
            for p in range(planes):
                value = window[planes + p]
                total = third[p * SIDE + 8 * t : p * SIDE + 8 * t + 8, :]
                shift = potential[base + p, pl.ds(8 * t, 8), :]
                if m <= DEGREE:
                    shift = shift - centre
                total = total + value * shift
                for j in range(1, REACH + 1):
                    around = window[planes + p + j] + window[planes + p - j]
                    above = field[base + planes + p, pl.ds(PAD + 8 * t + j, 8), :]
                    below = field[base + planes + p, pl.ds(PAD + 8 * t - j, 8), :]
                    total = total + weights[j] * (around + (above + below))
                yield base + planes + p, t, tile, value, total

    for m in range(1, DEGREE + 1):
        gain, back = recurrence[m - 1]
        low = max(0, m - (DEGREE + 1) + home)

        def block(k, carry, m=m, gain=gain, back=back):
            for plane, t, tile, _, total in apply(m, k):
                following = gain * total
                if back is not None:
                    following = following - back * fields[(m + 1) % 3][plane, tile, :]
                put(fields[m % 3], plane, t, following)
            return carry

        lax.fori_loop(low, blocks - low, block, 0)
        if m - DEGREE + home <= 0:
            wrap_planes(fields[m % 3])
    final = fields[DEGREE % 3]

    mine = planes + (home + core) * planes
    theirs = planes + (home + 1 - core) * planes
    body = pl.ds(PAD, SIDE)
    swap = remote(
        final.at[pl.ds(theirs, planes), body, :],
        out_ref.at[core],
        swap_sem.at[0],
        swap_sem.at[1],
        partner,
    )
    swap.start()

    def sums(k, carry):
        tops, bottoms = list(carry[0]), list(carry[1])
        for plane, t, _, value, total in apply(DEGREE + 1, k):
            tops[t % 2] = tops[t % 2] + value * total
            bottoms[t % 2] = bottoms[t % 2] + value * value
        return tuple(tops), tuple(bottoms)

    tops, bottoms = lax.fori_loop(home, blocks - home, sums, ((zero, zero), (zero, zero)))
    top, bottom = tops[0] + tops[1], bottoms[0] + bottoms[1]
    part[me, 0] = jnp.broadcast_to(jnp.sum(top, keepdims=True), (8, LANES))
    part[me, 1] = jnp.broadcast_to(jnp.sum(bottom, keepdims=True), (8, LANES))

    def reduction(d):
        return remote(
            part.at[me], part.at[me], send_red.at[d], recv_red.at[me], lax.rem(me + d, n)
        )

    for d in range(1, n):
        reduction(d).start()
    for i in range(planes):
        for t in range(TILES):
            out_ref[core, i, pl.ds(8 * t, 8), :] = final[mine + i, pl.ds(PAD + 8 * t, 8), :]
    for d in range(1, n):
        source = lax.rem(me + d, n)
        remote(
            part.at[source], part.at[source], send_red.at[d], recv_red.at[source], source
        ).wait_recv()
    kweight, fermi = kweight_ref[0], fermi_ref[0]
    term = zero
    for b in range(2):
        numerator, denominator = zero, zero
        for c in range(chips):
            numerator = numerator + part[2 * c + b, 0]
            denominator = denominator + part[2 * c + b, 1]
        energy = numerator / denominator
        energy_ref[b] = energy
        term = term + energy / (1.0 + jnp.exp((energy - fermi) / smearing))
    part_k[kpt] = kweight * term

    def across(d):
        return pltpu.make_async_remote_copy(
            src_ref=part_k.at[kpt],
            dst_ref=part_k.at[kpt],
            send_sem=send_k.at[d],
            recv_sem=recv_k.at[kpt],
            device_id=(lax.rem(kpt + d, members_k), me),
            device_id_type=MESH,
        )

    for d in range(1, members_k):
        across(d).start()
    for d in range(1, members_k):
        source = lax.rem(kpt + d, members_k)
        pltpu.make_async_remote_copy(
            src_ref=part_k.at[source],
            dst_ref=part_k.at[source],
            send_sem=send_k.at[d],
            recv_sem=recv_k.at[source],
            device_id=(source, me),
            device_id_type=MESH,
        ).wait_recv()
    grand = zero
    for k in range(members_k):
        grand = grand + part_k[k]
    total_ref[...] = grand

    swap.wait()
    for d in range(1, n):
        reduction(d).wait_send()
    for d in range(1, members_k):
        across(d).wait_send()

    @pl.when(has_up)
    def _():
        own(core, send.at[0], me + 2).wait_send()
        own(1 - core, send.at[1], partner + 2).wait_send()
        own_pot(send_pot.at[0], me + 2).wait_send()

    @pl.when(has_down)
    def _():
        own(core, send.at[2], me - 2).wait_send()
        own(1 - core, send.at[3], partner - 2).wait_send()
        own_pot(send_pot.at[1], me - 2).wait_send()

    own(1 - core, send.at[4], partner).wait_send()
    own_pot(send_pot.at[2], partner).wait_send()

    def drain(source, carry):
        @pl.when(source != chip)
        def _():
            onward = jnp.where(source < chip, has_up, has_down)
            target = jnp.where(source < chip, me + 2, me - 2)

            @pl.when(onward)
            def _():
                relay(2 * source, target).wait_send()
                relay(2 * source + 1, target).wait_send()
                relay_pot(2 * source + core, target, 0).wait_send()

            relay_pot(2 * source + core, partner, 1).wait_send()

        return carry

    lax.fori_loop(0, chips, drain, 0)


def per_device(bands, potential, table, kweight, lowest, cut, upper, fermi):
    n = lax.axis_size("grid")
    members_k = lax.axis_size("kpt")
    planes = bands.shape[3]
    parts = jnp.asarray(np.stack(third_parts()))

    waves = bands[0].reshape(2, 2, planes, SIDE, SIDE).transpose(1, 2, 3, 0, 4)
    waves = waves.reshape(2, 2 * planes, HALF, USED)
    head, tail = waves[:, :9], waves[:, 9:]
    tail = tail.reshape(2, 3, HALF, 3, 32).transpose(0, 1, 3, 2, 4).reshape(2, 9, HALF, 32)
    packed = jnp.concatenate([head, tail], axis=-1)

    pairs = potential.reshape(planes // 2, 2, SIDE, SIDE).transpose(0, 2, 1, 3)
    pairs = pairs.reshape(planes // 2, SIDE, USED)
    pairs = jnp.pad(pairs, ((0, 0), (0, 0), (0, LANES - USED)))

    vmem = pl.BlockSpec(memory_space=pltpu.VMEM)
    total_planes = n * planes
    dma = pltpu.SemaphoreType.DMA
    out, energy, total = pl.pallas_call(
        functools.partial(kernel, n, members_k),
        name="cheb",
        out_shape=(
            jax.ShapeDtypeStruct((2, planes, SIDE, LANES), jnp.float32),
            jax.ShapeDtypeStruct((2, 8, LANES), jnp.float32),
            jax.ShapeDtypeStruct((8, LANES), jnp.float32),
        ),
        in_specs=[pl.BlockSpec(memory_space=pltpu.SMEM)] * 6 + [vmem] * 3,
        out_specs=(vmem, vmem, vmem),
        scratch_shapes=[
            pltpu.VMEM((total_planes + 2 * planes, ROWS, LANES), jnp.float32),
            pltpu.VMEM((total_planes + 2 * planes, ROWS, LANES), jnp.float32),
            pltpu.VMEM((total_planes + 2 * planes, ROWS, LANES), jnp.float32),
            pltpu.VMEM((2 * LANES, 2 * LANES), jnp.bfloat16),
            pltpu.VMEM((total_planes, SIDE, LANES), jnp.float32),
            pltpu.VMEM((n, 9, HALF, LANES), jnp.float32),
            pltpu.VMEM((n, planes // 2, SIDE, LANES), jnp.float32),
            pltpu.VMEM((n, 2, 8, LANES), jnp.float32),
            pltpu.VMEM((members_k, 8, LANES), jnp.float32),
            dma((5 + n,)),
            dma((n,)),
            dma((3 + 2 * n,)),
            dma((n,)),
            dma((n,)),
            dma((n,)),
            dma((members_k,)),
            dma((members_k,)),
            dma((2,)),
        ],
        compiler_params=pltpu.CompilerParams(
            collective_id=0, has_side_effects=True, vmem_limit_bytes=56 * 1024 * 1024
        ),
    )(table, kweight, lowest, cut, upper, fermi, packed, pairs, parts)
    filtered = out[..., :USED].reshape(2, planes, SIDE, 2, SIDE).transpose(3, 0, 1, 2, 4)
    filtered = filtered.reshape(1, 2, 2, planes, SIDE * SIDE)
    return filtered, energy[:, 0, 0][None], total[0, :1]


def solution(mesh):
    in_specs = (
        P("kpt", None, None, "grid", None),
        P("grid", None),
        P("kpt", None),
        P("kpt"),
        P("kpt"),
        P("kpt"),
        P("kpt"),
        P(),
    )
    out_specs = (P("kpt", None, None, "grid", None), P("kpt", None), P())
    return jax.shard_map(
        per_device, mesh=mesh, in_specs=in_specs, out_specs=out_specs, check_vma=False
    )
```

profile of v0, /device:TPU:0, one launch (start us, length us, event | category | flops | bytes accessed | tf_op | source)
XLA Modules:
  0.0 71.2 jit_solution(9591200044052813113)
XLA Ops:
  0.6 1.3 %reshape_squeeze.3 = f32[2,2,6,48,48]{4,3,1,2,0:T(8,128)S(1)} reshape(f32[1,2,2,6,2304]{4,2,3,1,0:T(2,128)} %param.9) | data formatting | bytes 442368 | tf_op jit(solution)/shard_map/reshape;squeeze | solution.py:535
  2.0 0.5 copy.30
  2.4 0.3 reshape.25
  2.8 0.1 fusion
  2.9 0.0 copy-start
  2.9 0.8 %pad_maximum_fusion.1.packed_ref = f32[2,9,24,128]{3,2,1,0:T(8,128)} fusion(f32[2,9,24,32]{3,2,1,0:T(8,128)S(1)} %bitcast.21, f32[2,9,24,96]{3,2,1,0:T(8,128)S(1)} %slice.32), kind=kLoop, calls=%fused_computation.2 | loop fusion | flops 55296 | bytes 442368 | tf_op jit(solution)/shard_map/concatenate | solution.py:539
  3.8 0.1 copy-done
  3.8 0.1 reshape.27
  3.9 0.1 copy.31
  4.0 0.1 reshape.28
  4.2 0.7 pad.4.pot_ref
  8.1 58.2 %cheb.1 = (f32[2,6,48,128]{3,2,1,0:T(8,128)}, f32[2,8,128]{2,1,0:T(8,128)}, f32[8,128]{1,0:T(8,128)}) custom-call(s32[1,3]{1,0:T(1,128)} %table_ref.1, f32[1]{0:T(128)S(6)} %copy.32.kweight_ref, f32[1]{0:T(128)S(6)} %copy.33.lowest_ref, f32[1]{0:T(128)S(6)} %copy.34.cut_ref, f32[1]{0:T(128)S(6)} %copy.35.upper_ref, f32[1]{0:T(128)S(6)} %copy.36.fermi_ref, ...), custom_call_target="tpu_custom_call" | custom-call | tf_op jit(solution)/shard_map/cheb/pallas_call | solution.py:548
  66.2 1.3 %reshape.29 = f32[2,6,48,2,48]{4,3,2,1,0:T(2,128)S(1)} reshape(f32[2,6,48,96]{3,2,1,0:T(8,128)} %bitcast.23) | data formatting | bytes 442368 | tf_op jit(solution)/shard_map/reshape | solution.py:582
  67.6 1.1 %reshape.30 = f32[1,2,2,6,2304]{4,2,3,1,0:T(2,128)} reshape(f32[2,2,6,48,48]{4,3,1,2,0:T(8,128)S(1)} %copy.27) | data formatting | bytes 442368 | tf_op jit(solution)/shard_map/reshape | solution.py:583
  68.7 1.2 %slice.31 = f32[1,1]{1,0:T(1,128)} slice(f32[8,128]{1,0:T(8,128)} %get-tuple-element.8), slice={[0:1], [0:1]} | slice | bytes 8 | tf_op jit(solution)/shard_map/slice | solution.py:584
  69.9 1.3 %slice_reduce_fusion = f32[2]{0:T(128)} fusion(f32[2,8,128]{2,1,0:T(8,128)} %get-tuple-element.7), kind=kLoop, calls=%fused_computation.4 | loop fusion | bytes 16 | tf_op jit(solution)/shard_map/slice | solution.py:584
  (3 shorter events, 0.1 us)
Async XLA Ops:
  2.9 0.9 %copy-start = (f32[6,2304]{1,0:T(8,128)S(1)}, f32[6,2304]{1,0:T(8,128)}, u32[]{:S(2)}) copy-start(f32[6,2304]{1,0:T(8,128)} %param.10) | copy-start | bytes 165892
where the time goes:
time: 71.6 us; the launch traced here: 71.2 us
  Pallas kernels  58.2 us (81%)
  local copies, waits for them, and re-layouts  8.25 us (12%)
  between operations  3.97 us (6%)
  other arithmetic  0.83 us (1%)
    pallas_call x1, Pallas kernels, per_device(): pl.pallas_call(functools.partial(kernel, n, members_k), name='cheb', out_...  58.2 us
    slice x2, local copies, waits for them, and re-layouts, per_device(): return (filtered, energy[:, 0, 0][None], total[0, :1])  2.49 us
    another operation x2, local copies, waits for them, and re-layouts, per_device(): waves = bands[0].reshape(2, 2, planes, SIDE, SIDE).transpose(1, 2, 3, 0, 4)  1.79 us

commit v1 on v0

v1 whole, which is shorter than its diff:
```python
import functools

import jax
import jax.numpy as jnp
import numpy as np
from jax import lax
from jax.experimental import pallas as pl
from jax.experimental.layout import Layout, with_layout_constraint
from jax.experimental.pallas import tpu as pltpu
from jax.sharding import PartitionSpec as P

SIDE = 48
DEGREE = 6
PHASE_DIVISOR = 8
REACH = 6
LANES = 128
USED = 2 * SIDE
PAD = 8
ROWS = SIDE + 2 * PAD
TILES = SIDE // 8
CHUNKS = SIDE * SIDE // LANES
PER_TILE = CHUNKS // TILES
BANDS = 2

coefficients = (
    -5369.0 / 1800.0,
    12.0 / 7.0,
    -15.0 / 56.0,
    10.0 / 189.0,
    -1.0 / 112.0,
    2.0 / 1925.0,
    -1.0 / 16632.0,
)
smearing = 0.5
MESH = pl.DeviceIdType.MESH


def third_parts():
    inside = np.zeros((SIDE, SIDE))
    over = np.zeros((SIDE, SIDE))
    under = np.zeros((SIDE, SIDE))
    for z in range(SIDE):
        for j in range(1, REACH + 1):
            weight = -0.5 * coefficients[j]
            for target, sign in ((z + j, 1), (z - j, -1)):
                if 0 <= target < SIDE:
                    inside[target, z] += weight
                elif sign > 0:
                    over[target - SIDE, z] += weight
                else:
                    under[target + SIDE, z] += weight
    plain = np.zeros((LANES, LANES))
    cosine = np.zeros((LANES, LANES))
    sine = np.zeros((LANES, LANES))
    both, apart = over + under, over - under
    for c in range(2):
        s = slice(c * SIDE, (c + 1) * SIDE)
        plain[s, s] = inside
        cosine[s, s] = both
    re, im = slice(0, SIDE), slice(SIDE, USED)
    sine[im, re] = -apart
    sine[re, im] = apart
    return [a.astype(np.float32) for a in (plain, cosine, sine)]


def kernel(
    n,
    members_k,
    planes,
    table_hbm,
    kweight_hbm,
    lowest_hbm,
    cut_hbm,
    upper_hbm,
    fermi_hbm,
    bands_hbm,
    pot_hbm,
    parts_hbm,
    out_ref,
    energy_ref,
    total_ref,
    table_ref,
    kweight_ref,
    lowest_ref,
    cut_ref,
    upper_ref,
    fermi_ref,
    own,
    own_pot,
    parts_ref,
    field_0,
    field_1,
    field_2,
    mat_ref,
    potential,
    stage,
    stage_pot,
    turned,
    rolled,
    packed,
    part,
    part_k,
    load_sem,
    send,
    recv,
    send_pot,
    recv_pot,
    halo_send,
    halo_recv,
    out_send,
    out_recv,
    send_red,
    recv_red,
    send_k,
    recv_k,
):
    fields = (field_0, field_1, field_2)
    chips = n // 2
    slabs = n // 2
    total_planes = slabs * planes
    first_worker = 2 * (chips // 2 - 1)
    workers = 2 * BANDS
    me = lax.axis_index("grid")
    kpt = lax.axis_index("kpt")
    core = lax.rem(me, 2)
    partner = me + 1 - 2 * core
    is_worker = (me >= first_worker) & (me < first_worker + workers)
    my_band = lax.div(me - first_worker, 2)
    my_half = lax.div(me, slabs)
    my_slot = lax.rem(me, slabs)

    loads = [
        pltpu.make_async_copy(src, dst, load_sem.at[i])
        for i, (src, dst) in enumerate(
            (
                (table_hbm, table_ref),
                (kweight_hbm, kweight_ref),
                (lowest_hbm, lowest_ref),
                (cut_hbm, cut_ref),
                (upper_hbm, upper_ref),
                (fermi_hbm, fermi_ref),
                (parts_hbm, parts_ref),
                (pot_hbm, own_pot),
                (bands_hbm.at[:, 0], own.at[0]),
                (bands_hbm.at[:, 1], own.at[1]),
            )
        )
    ]
    for load in loads[::-1]:
        load.start()

    barrier = pltpu.get_barrier_semaphore()

    def greet(target_k, target):
        pl.semaphore_signal(barrier, inc=1, device_id=(target_k, target), device_id_type=MESH)

    for d in range(1, members_k):
        greet(lax.rem(kpt + d, members_k), me)

    @pl.when(is_worker)
    def _():
        for d in range(1, n):
            greet(kpt, lax.rem(me + d, n))

    @pl.when(jnp.logical_not(is_worker))
    def _():
        for w in range(workers):
            greet(kpt, first_worker + w)

    loads[7].wait()
    loads[8].wait()
    loads[9].wait()
    pl.semaphore_wait(
        barrier, jnp.where(is_worker, n - 1 + members_k - 1, workers + members_k - 1)
    )

    def remote(src, dst, ssem, rsem, target):
        return pltpu.make_async_remote_copy(
            src_ref=src,
            dst_ref=dst,
            send_sem=ssem,
            recv_sem=rsem,
            device_id=(kpt, target),
            device_id_type=MESH,
        )

    def deliver(i):
        b = 1 - my_half if i == 0 else my_half
        target = first_worker + 2 * b + my_half
        wave = remote(own.at[b], stage.at[my_slot], send.at[i], recv.at[my_slot], target)
        pot = remote(own_pot, stage_pot.at[my_slot], send_pot.at[i], recv_pot.at[my_slot], target)
        return wave, pot, target

    for i in range(BANDS):
        wave, pot, target = deliver(i)

        @pl.when(target != me)
        def _():
            wave.start()
            pot.start()

    lane = lax.broadcasted_iota(jnp.int32, (8, LANES), 1)
    row = lax.broadcasted_iota(jnp.int32, (8, LANES), 0)
    first = lane < SIDE
    used = lane < USED
    zero = jnp.zeros((8, LANES), jnp.float32)

    def turn(v, cosine, sine):
        other = jnp.where(first, pltpu.roll(v, LANES - SIDE, 1), pltpu.roll(v, SIDE, 1))
        signed = jnp.where(used, jnp.where(first, -sine, sine), 0.0)
        return cosine * v + signed * other

    def spread(scalar):
        return jnp.full((8, LANES), scalar)

    for i in range(7):
        loads[i].wait()

    low_end, cut_end, high_end = (spread(r[0]) for r in (lowest_ref, cut_ref, upper_ref))
    half_width = (high_end - cut_end) / 2.0
    centre = (high_end + cut_end) / 2.0

    @pl.when(is_worker)
    def _():
        def phase(d):
            numerator = spread(table_ref[0, d])
            cosine, sine = jnp.ones((8, LANES), jnp.float32), zero
            for i in range(1, PHASE_DIVISOR):
                here = numerator == i
                angle = 2.0 * np.pi * i / PHASE_DIVISOR
                cosine = jnp.where(here, float(np.cos(angle)), cosine)
                sine = jnp.where(here, float(np.sin(angle)), sine)
            return cosine, sine

        cos_x, sin_x = phase(0)
        cos_y, sin_y = phase(1)
        cos_z, sin_z = phase(2)
        at_low = spread(core) == 0
        side_turn = (
            (jnp.where(at_low, cos_x, 1.0), jnp.where(at_low, sin_x, 0.0)),
            (jnp.where(at_low, 1.0, cos_x), jnp.where(at_low, 0.0, -sin_x)),
        )
        first_sigma = half_width / (low_end - centre)
        sigma = first_sigma
        final_scale = first_sigma
        for degree in range(1, DEGREE):
            sigma = 1.0 / (2.0 / first_sigma - sigma)
            final_scale = final_scale * sigma
        scale = 2.0 / half_width
        weights = [scale * (-0.5 * c) for c in coefficients]

        for r in range(LANES // 16):
            rows = pl.ds(16 * r, 16)
            cosine = jnp.concatenate([cos_z, cos_z], axis=0)
            sine = jnp.concatenate([sin_z, sin_z], axis=0)
            entry = (
                parts_ref[0, rows, :] + cosine * parts_ref[1, rows, :] + sine * parts_ref[2, rows, :]
            )
            entry = entry * jnp.concatenate([scale, scale], axis=0)
            high = entry.astype(jnp.bfloat16)
            rest = (entry - high.astype(jnp.float32)).astype(jnp.bfloat16)
            lower = pl.ds(LANES + 16 * r, 16)
            mat_ref[rows, pl.ds(0, LANES)] = high
            mat_ref[rows, pl.ds(LANES, LANES)] = rest
            mat_ref[lower, pl.ds(0, LANES)] = high
            mat_ref[lower, pl.ds(LANES, LANES)] = jnp.zeros_like(high)

        def clear(p, carry):
            for t in range(TILES):
                field_2[planes + p, pl.ds(PAD + 8 * t, 8), :] = zero
            return carry

        lax.fori_loop(0, total_planes, clear, 0)

        def put(f, plane, t, v):
            f[plane, pl.ds(PAD + 8 * t, 8), :] = v
            if t == 0:
                f[plane, pl.ds(PAD + SIDE, 8), :] = turn(v, cos_y, sin_y)
            if t == TILES - 1:
                f[plane, pl.ds(0, 8), :] = turn(v, cos_y, -sin_y)

        def ordering(part_index):
            begin = SIDE * lax.rem(5 * row + part_index, 8)
            which = lax.shift_right_logical(begin + ((lane - begin) & (LANES - 1)), 7)
            return which, lax.rem(5 * row + 3 * part_index, 8)

        orders = [ordering(i) for i in range(2)]

        def lay(load, part_index):
            which, back = orders[part_index]
            ahead = [jnp.broadcast_to(load(i), (8, LANES)) for i in range(PER_TILE)]
            v = jnp.where(which == 0, ahead[0], jnp.where(which == 1, ahead[1], ahead[2]))
            v = pltpu.roll(v, 0, 1, stride=16, stride_axis=0)
            return jnp.take_along_axis(v, back, axis=0)

        flat = stage.reshape(slabs, 2 * planes * CHUNKS, LANES)

        def unpack(slot):
            for p in range(planes):
                for t in range(TILES):
                    def rows_of(part_index):
                        base = (part_index * planes + p) * CHUNKS + PER_TILE * t
                        return lay(
                            lambda i: flat[slot, pl.ds(base + i, 1), :], part_index
                        )

                    v = jnp.where(first, rows_of(0), jnp.where(used, rows_of(1), 0.0))
                    put(field_0, planes + slot * planes + p, t, v)

        def unpack_pot(slot):
            for p in range(planes):
                for t in range(TILES):
                    v = lay(
                        lambda i: stage_pot[
                            slot, pl.ds(p, 1), pl.ds((PER_TILE * t + i) * LANES, LANES)
                        ],
                        0,
                    )
                    v = (v - 1.5 * coefficients[0] - centre) * scale
                    v = jnp.where(first, v, jnp.where(used, pltpu.roll(v, SIDE, 1), 0.0))
                    potential[slot * planes + p, pl.ds(8 * t, 8), :] = v

        def take(i, carry):
            slot = jnp.where(core == 0, slabs - 1 - i, i)

            @pl.when(half_base + slot != me)
            def _():
                remote(stage.at[slot], stage.at[slot], send.at[0], recv.at[slot], partner).wait_recv()
                remote(
                    stage_pot.at[slot], stage_pot.at[slot], send_pot.at[0], recv_pot.at[slot], partner
                ).wait_recv()

            unpack(slot)
            unpack_pot(slot)
            return carry

        half_base = core * slabs

        @pl.when(my_half == core)
        def _():
            own_flat = own.reshape(BANDS, 2 * planes * CHUNKS, LANES)
            for r in range(2 * planes * CHUNKS // 8):
                flat[my_slot, pl.ds(8 * r, 8), :] = own_flat[my_band, pl.ds(8 * r, 8), :]
            for c in range(CHUNKS):
                part_of = pl.ds(c * LANES, LANES)
                stage_pot[my_slot, :, part_of] = own_pot[:, part_of]

        lax.fori_loop(0, slabs, take, 0)

        body = pl.ds(PAD, SIDE)

        def halo(f, side, parity):
            there = total_planes + planes if side == 0 else 0
            return remote(
                turned.at[side],
                f.at[pl.ds(there, planes), body, :],
                halo_send.at[side],
                halo_recv.at[1 - side, parity],
                partner,
            )

        def hold(side, p, t, v):
            turned[side, p, pl.ds(8 * t, 8), :] = turn(v, *side_turn[side])

        for side in range(2):
            base = planes if side == 0 else total_planes

            for p in range(planes):
                for t in range(TILES):
                    hold(side, p, t, field_0[base + p, pl.ds(PAD + 8 * t, 8), :])
            halo(field_0, side, 0).start()

        def apply(f, k):
            base = k * planes
            middle = [f[base + planes + p, body, :] for p in range(planes)]
            rows = jnp.concatenate(middle, axis=0)
            high = rows.astype(jnp.bfloat16)
            rest = (rows - high.astype(jnp.float32)).astype(jnp.bfloat16)
            both = jnp.concatenate([high, rest], axis=1)
            third = jnp.dot(both, mat_ref[...], preferred_element_type=jnp.float32)
            third = third[:, :LANES] + third[:, LANES:]
            for t in range(TILES):
                tile = pl.ds(PAD + 8 * t, 8)
                window = [f[base + i, tile, :] for i in range(3 * planes)]
                for p in range(planes):
                    value = window[planes + p]
                    total = third[p * SIDE + 8 * t : p * SIDE + 8 * t + 8, :]
                    total = total + value * potential[base + p, pl.ds(8 * t, 8), :]
                    for j in range(1, REACH + 1):
                        around = window[planes + p + j] + window[planes + p - j]
                        above = f[base + planes + p, pl.ds(PAD + 8 * t + j, 8), :]
                        below = f[base + planes + p, pl.ds(PAD + 8 * t - j, 8), :]
                        total = total + weights[j] * (around + (above + below))
                    yield p, base + planes + p, t, tile, value, total

        def await_halos(f, parity):
            for side in range(2):
                halo(f, side, parity).wait_send()
            for side in range(2):
                there = total_planes + planes if side == 1 else 0
                landed = f.at[pl.ds(there, planes), body, :]
                remote(
                    landed, landed, halo_send.at[side], halo_recv.at[side, parity], partner
                ).wait_recv()

        def step(m, c):
            now, then, before = (fields[(c + i) % 3] for i in range(3))
            gain = jnp.where(m == 1, 0.5, 1.0)

            def block(k, side=None):
                for p, plane, t, tile, _, total in apply(now, k):
                    following = gain * total - before[plane, tile, :]
                    put(then, plane, t, following)
                    if side is not None:
                        hold(side, p, t, following)

            def inner(k, carry):
                block(k)
                return carry

            lax.fori_loop(1, slabs - 1, inner, 0)
            parity = lax.rem(m - 1, 2)
            await_halos(now, parity)
            block(0, 0)
            halo(then, 0, 1 - parity).start()
            block(slabs - 1, 1)
            halo(then, 1, 1 - parity).start()

        def three(r, carry):
            for c in range(3):
                step(3 * r + c + 1, c)
            return carry

        lax.fori_loop(0, DEGREE // 3, three, 0)
        final = field_0

        flat_packed = packed.reshape(slabs, 2 * planes * CHUNKS, LANES)
        gather_rows = [lax.rem(3 * row + i, 8) for i in range(2)]
        lane6 = lax.broadcasted_iota(jnp.int32, (TILES, LANES), 1)

        def give(slot):
            return remote(
                packed.at[slot],
                out_ref.at[:, my_band],
                out_send.at[slot],
                out_recv.at[my_band],
                core * slabs + slot,
            )

        def give_here(slot):
            return pltpu.make_async_copy(
                packed.at[slot], out_ref.at[:, my_band], out_recv.at[my_band]
            )

        def pack(i, carry):
            slot = jnp.where(core == 0, i, slabs - 1 - i)

            for p in range(planes):
                plane = planes + slot * planes + p
                for part_index in range(2):
                    lot = 2 * p + part_index
                    for t in range(TILES):
                        v = final[plane, pl.ds(PAD + 8 * t, 8), :] * final_scale
                        v = jnp.take_along_axis(v, gather_rows[part_index], axis=0)
                        v = pltpu.roll(v, 0, 1, stride=16, stride_axis=0)
                        rolled[lot, pl.ds(8 * t, 8), :] = v
            for p in range(planes):
                for part_index in range(2):
                    lot = 2 * p + part_index
                    picks = [
                        rolled[lot, pl.ds((3 * i + 5 * part_index) % 8, TILES, stride=8), :]
                        for i in range(8)
                    ]

                    def choose(*ends):
                        start = ends[0]
                        v = picks[start + len(ends) - 1]
                        for i in range(len(ends) - 2, -1, -1):
                            v = jnp.where(lane6 < ends[i + 1], picks[start + i], v)
                        return v

                    rows = (choose(0, 48, 96), choose(2, 16, 64, 112), choose(5, 32, 80))
                    base = (part_index * planes + p) * CHUNKS
                    for j in range(PER_TILE):
                        flat_packed[slot, pl.ds(base + j, TILES, stride=PER_TILE), :] = rows[j]

            @pl.when(core * slabs + slot != me)
            def _():
                give(slot).start()

            @pl.when(core * slabs + slot == me)
            def _():
                give_here(slot).start()

            return carry

        lax.fori_loop(0, slabs, pack, 0)

        def sums(k, carry):
            tops, bottoms = list(carry[0]), list(carry[1])
            for _, _, t, _, value, total in apply(final, k):
                tops[t % 2] = tops[t % 2] + value * total
                bottoms[t % 2] = bottoms[t % 2] + value * value
            return tuple(tops), tuple(bottoms)

        carry = ((zero, zero), (zero, zero))
        carry = lax.fori_loop(1, slabs - 1, sums, carry)
        await_halos(final, DEGREE % 2)
        carry = sums(0, carry)
        tops, bottoms = sums(slabs - 1, carry)
        top = jnp.sum(tops[0] + tops[1], keepdims=True)
        bottom = jnp.sum(bottoms[0] + bottoms[1], keepdims=True)
        left = lax.broadcasted_iota(jnp.int32, (1, LANES), 1) < LANES // 2
        part[me - first_worker] = jnp.where(left, top, bottom)
        for d in range(1, n):
            remote(
                part.at[me - first_worker],
                part.at[me - first_worker],
                send_red.at[d],
                recv_red.at[me - first_worker],
                lax.rem(me + d, n),
            ).start()

    for w in range(workers):

        @pl.when(me != first_worker + w)
        def _():
            remote(part.at[w], part.at[w], send_red.at[0], recv_red.at[w], first_worker + w).wait_recv()

    kweight, fermi = kweight_ref[0], fermi_ref[0]
    e_half, c_half = half_width[0:1, :], centre[0:1, :]
    term = jnp.zeros((1, LANES), jnp.float32)
    for b in range(BANDS):
        both = part[2 * b] + part[2 * b + 1]
        energy = (0.5 * e_half) * (both / pltpu.roll(both, LANES // 2, 1)) + c_half
        energy_ref[0, b] = energy[0, 0]
        term = term + energy / (1.0 + jnp.exp((energy - fermi) / smearing))
    part_k[kpt] = kweight * term

    def across(d, source, target):
        return pltpu.make_async_remote_copy(
            src_ref=part_k.at[source],
            dst_ref=part_k.at[source],
            send_sem=send_k.at[d],
            recv_sem=recv_k.at[source],
            device_id=(target, me),
            device_id_type=MESH,
        )

    for d in range(1, members_k):
        across(d, kpt, lax.rem(kpt + d, members_k)).start()
    for d in range(1, members_k):
        source = lax.rem(kpt + d, members_k)
        across(d, source, source).wait_recv()
    grand = jnp.zeros((1, LANES), jnp.float32)
    for k in range(members_k):
        grand = grand + part_k[k]
    total_ref[0, 0] = grand[0, 0]

    for b in range(BANDS):
        landing = out_ref.at[:, b]
        remote(landing, landing, out_send.at[0], out_recv.at[b], partner).wait_recv()

    for i in range(BANDS):
        wave, pot, target = deliver(i)

        @pl.when(target != me)
        def _():
            wave.wait_send()
            pot.wait_send()

    for d in range(1, members_k):
        across(d, kpt, lax.rem(kpt + d, members_k)).wait_send()

    @pl.when(is_worker)
    def _():
        for d in range(1, n):
            remote(
                part.at[me - first_worker],
                part.at[me - first_worker],
                send_red.at[d],
                recv_red.at[me - first_worker],
                lax.rem(me + d, n),
            ).wait_send()

        def drain(slot, carry):
            @pl.when(core * slabs + slot != me)
            def _():
                remote(
                    packed.at[slot],
                    out_ref.at[:, my_band],
                    out_send.at[slot],
                    out_recv.at[my_band],
                    core * slabs + slot,
                ).wait_send()

            return carry

        lax.fori_loop(0, slabs, drain, 0)


def per_device(bands, potential, table, kweight, lowest, cut, upper, fermi):
    n = lax.axis_size("grid")
    members_k = lax.axis_size("kpt")
    planes = bands.shape[3]
    parts = jnp.asarray(np.stack(third_parts()))
    pieces = 2 * planes
    flat = pieces * CHUNKS

    raw = bands[0].transpose(0, 2, 1, 3).reshape(pieces, BANDS, CHUNKS, LANES)
    raw = with_layout_constraint(raw, Layout((0, 2, 1, 3)))
    raw = raw.transpose(0, 2, 1, 3).reshape(flat, BANDS, 1, LANES)

    vmem, smem = pltpu.VMEM, pltpu.SMEM
    anywhere = pl.BlockSpec(memory_space=pl.ANY)
    hbm = pl.BlockSpec(memory_space=pltpu.HBM)
    scalar = pl.BlockSpec(memory_space=smem)
    slabs = n // 2
    workers = 2 * BANDS
    total_planes = slabs * planes
    dma = pltpu.SemaphoreType.DMA
    f32 = jnp.float32
    out, energy, total = pl.pallas_call(
        functools.partial(kernel, n, members_k, planes),
        name="cheb",
        out_shape=(
            jax.ShapeDtypeStruct((flat, BANDS, 1, LANES), f32),
            jax.ShapeDtypeStruct((1, BANDS), f32),
            jax.ShapeDtypeStruct((1, 1), f32),
        ),
        in_specs=[anywhere] * 6 + [hbm] * 3,
        out_specs=(hbm, scalar, scalar),
        scratch_shapes=[
            smem((1, 3), jnp.int32),
            smem((1,), f32),
            smem((1,), f32),
            smem((1,), f32),
            smem((1,), f32),
            smem((1,), f32),
            vmem((BANDS, flat, 1, LANES), f32),
            vmem((planes, SIDE * SIDE), f32),
            vmem((3, LANES, LANES), f32),
            vmem((total_planes + 2 * planes, ROWS, LANES), f32),
            vmem((total_planes + 2 * planes, ROWS, LANES), f32),
            vmem((total_planes + 2 * planes, ROWS, LANES), f32),
            vmem((2 * LANES, 2 * LANES), jnp.bfloat16),
            vmem((total_planes, SIDE, LANES), f32),
            vmem((slabs, flat, 1, LANES), f32),
            vmem((slabs, planes, SIDE * SIDE), f32),
            vmem((2, planes, SIDE, LANES), f32),
            vmem((2 * planes, SIDE, LANES), f32),
            vmem((slabs, flat, 1, LANES), f32),
            vmem((workers, 1, LANES), f32),
            vmem((members_k, 1, LANES), f32),
            dma((10,)),
            dma((BANDS,)),
            dma((slabs,)),
            dma((BANDS,)),
            dma((slabs,)),
            dma((2,)),
            dma((2, 2)),
            dma((slabs,)),
            dma((BANDS,)),
            dma((n,)),
            dma((workers,)),
            dma((members_k,)),
            dma((members_k,)),
        ],
        compiler_params=pltpu.CompilerParams(
            collective_id=0, has_side_effects=True, vmem_limit_bytes=48 * 1024 * 1024
        ),
    )(table, kweight, lowest, cut, upper, fermi, raw, potential, parts)
    filtered = out.reshape(pieces, CHUNKS, BANDS, LANES).transpose(0, 2, 1, 3)
    filtered = filtered.reshape(2, planes, BANDS, SIDE * SIDE).transpose(0, 2, 1, 3)[None]
    return filtered, energy, total[0]


def solution(mesh):
    in_specs = (
        P("kpt", None, None, "grid", None),
        P("grid", None),
        P("kpt", None),
        P("kpt"),
        P("kpt"),
        P("kpt"),
        P("kpt"),
        P(),
    )
    out_specs = (P("kpt", None, None, "grid", None), P("kpt", None), P())
    return jax.shard_map(
        per_device, mesh=mesh, in_specs=in_specs, out_specs=out_specs, check_vma=False
    )
```

time: 71.6 us -> 53.5 us (0.75)
  Pallas kernels: 58.2 us -> 43 us
  local copies, waits for them, and re-layouts: 8.25 us -> 4.59 us
  between operations: 3.97 us -> 5.63 us
  other arithmetic: 0.83 us -> 0 us
    pallas_call x1, Pallas kernels: 58.2 us -> 43 us  [per_device(): pl.pallas_call(functools.partial(kernel, n, members_k, planes), name='che...]
    unnamed x2 -> x10, local copies, waits for them, and re-layouts: 0.06 us -> 4.59 us
    reshape x6 -> x0, local copies, waits for them, and re-layouts: 3.1 us -> none  [the longest x1 1.32 us: per_device(): out[..., :USED].reshape(2, planes, SIDE, 2, SIDE).transpose(3, 0, 1, 2, 4)]
    slice x4 -> x0, local copies, waits for them, and re-layouts: 2.6 us -> none  [the longest x2 2.49 us: per_device(): return (filtered, energy[:, 0, 0][None], total[0, :1])]
    another operation x2 -> x0, local copies, waits for them, and re-layouts: 1.79 us -> none  [per_device(): waves = bands[0].reshape(2, 2, planes, SIDE, SIDE).transpose(1, 2, 3, 0, 4)]
    concatenate x2 -> x0, other arithmetic: 0.83 us -> none  [the longest x1 0.81 us: per_device(): packed = jnp.concatenate([head, tail], axis=-1)]
where the time goes in v1:
time: 53.5 us; the launch traced here: 53.2 us
  Pallas kernels  43 us (80%)
  between operations  5.63 us (11%)
  local copies, waits for them, and re-layouts  4.59 us (9%)
    pallas_call x1, Pallas kernels, per_device(): pl.pallas_call(functools.partial(kernel, n, members_k, planes), name='che...  43 us
    unnamed x10, local copies, waits for them, and re-layouts  4.59 us

profile of v1, /device:TPU:0, one launch (start us, length us, event | category | flops | bytes accessed | tf_op | source)
XLA Modules:
  0.0 53.2 jit_solution(9851622780539406198)
XLA Ops:
  3.9 0.0 copy-start.3
  3.9 0.6 %copy-done.3 = s32[1,3]{1,0:T(1,128)S(1)} copy-done((s32[1,3]{1,0:T(1,128)S(1)}, s32[1,3]{1,0:T(1,128)}, u32[]{:S(2)}) %copy-start.3) | copy-done | bytes 36
  4.5 0.0 copy-start
  4.5 0.9 %copy-done = f32[1,2,2,6,2304]{4,2,3,1,0:T(2,128)S(1)} copy-done((f32[1,2,2,6,2304]{4,2,3,1,0:T(2,128)S(1)}, f32[1,2,2,6,2304]{4,2,3,1,0:T(2,128)}, u32[]{:S(2)}) %copy-start) | copy-done | bytes 221208
  5.5 0.0 copy-start.1
  5.5 0.9 %copy-done.1 = f32[3,128,128]{2,1,0:T(8,128)S(1)} copy-done((f32[3,128,128]{2,1,0:T(8,128)S(1)}, f32[3,128,128]{2,1,0:T(8,128)}, u32[]{:S(2)}) %copy-start.1) | copy-done | bytes 196632
  6.4 0.0 copy-start.2
  6.4 0.9 %copy-done.2 = f32[6,2304]{1,0:T(8,128)S(1)} copy-done((f32[6,2304]{1,0:T(8,128)S(1)}, f32[6,2304]{1,0:T(8,128)}, u32[]{:S(2)}) %copy-start.2) | copy-done | bytes 55320
  7.3 43.0 %cheb.1 = (f32[216,2,1,128]{3,2,1,0:T(1,128)S(1)}, f32[1,2]{1,0:T(1,128)S(1)}, f32[1,1]{1,0:T(1,128)}) custom-call(s32[1,3]{1,0:T(1,128)S(1)} %copy-done.3, f32[1]{0:T(128)S(6)} %copy.15.kweight_hbm, f32[1]{0:T(128)S(6)} %copy.16.lowest_hbm, f32[1]{0:T(128)S(6)} %copy.17.cut_hbm, f32[1]{0:T(128)S(6)} %copy.18.upper_hbm, f32[1]{0:T(128)S(6)} %copy.19.fermi_hbm, ...), custom_call_target="tpu_custom_call" | custom-call | tf_op jit(solution)/shard_map/cheb/pallas_call | solution.py:623
  50.3 0.7 %copy.20 = f32[1,2,2,6,2304]{4,2,3,1,0:T(2,128)} copy(f32[1,2,2,6,2304]{4,2,3,1,0:T(2,128)S(1)} %bitcast.19) | data formatting | bytes 442368
  51.0 0.5 copy.21
Async XLA Ops:
  3.9 0.7 %copy-start.3 = (s32[1,3]{1,0:T(1,128)S(1)}, s32[1,3]{1,0:T(1,128)}, u32[]{:S(2)}) copy-start(s32[1,3]{1,0:T(1,128)} %table_hbm.1) | copy-start | bytes 40
  4.5 0.9 %copy-start = (f32[1,2,2,6,2304]{4,2,3,1,0:T(2,128)S(1)}, f32[1,2,2,6,2304]{4,2,3,1,0:T(2,128)}, u32[]{:S(2)}) copy-start(f32[1,2,2,6,2304]{4,2,3,1,0:T(2,128)} %param.9) | copy-start | bytes 663556
  5.5 0.9 %copy-start.1 = (f32[3,128,128]{2,1,0:T(8,128)S(1)}, f32[3,128,128]{2,1,0:T(8,128)}, u32[]{:S(2)}) copy-start(f32[3,128,128]{2,1,0:T(8,128)} %constant.2.clone.parts_hbm) | copy-start | bytes 589828
  6.4 0.9 %copy-start.2 = (f32[6,2304]{1,0:T(8,128)S(1)}, f32[6,2304]{1,0:T(8,128)}, u32[]{:S(2)}) copy-start(f32[6,2304]{1,0:T(8,128)} %pot_hbm.1) | copy-start | bytes 165892

commit v2 on v1

--- a/solution.py
+++ b/solution.py
@@ -35,39 +35,11 @@
 MESH = pl.DeviceIdType.MESH
 
 
-def third_parts():
-    inside = np.zeros((SIDE, SIDE))
-    over = np.zeros((SIDE, SIDE))
-    under = np.zeros((SIDE, SIDE))
-    for z in range(SIDE):
-        for j in range(1, REACH + 1):
-            weight = -0.5 * coefficients[j]
-            for target, sign in ((z + j, 1), (z - j, -1)):
-                if 0 <= target < SIDE:
-                    inside[target, z] += weight
-                elif sign > 0:
-                    over[target - SIDE, z] += weight
-                else:
-                    under[target + SIDE, z] += weight
-    plain = np.zeros((LANES, LANES))
-    cosine = np.zeros((LANES, LANES))
-    sine = np.zeros((LANES, LANES))
-    both, apart = over + under, over - under
-    for c in range(2):
-        s = slice(c * SIDE, (c + 1) * SIDE)
-        plain[s, s] = inside
-        cosine[s, s] = both
-    re, im = slice(0, SIDE), slice(SIDE, USED)
-    sine[im, re] = -apart
-    sine[re, im] = apart
-    return [a.astype(np.float32) for a in (plain, cosine, sine)]
-
-
 def kernel(
     n,
     members_k,
     planes,
-    table_hbm,
+    table_ref,
     kweight_hbm,
     lowest_hbm,
     cut_hbm,
@@ -75,11 +47,9 @@
     fermi_hbm,
     bands_hbm,
     pot_hbm,
-    parts_hbm,
     out_ref,
     energy_ref,
     total_ref,
-    table_ref,
     kweight_ref,
     lowest_ref,
     cut_ref,
@@ -87,15 +57,16 @@
     fermi_ref,
     own,
     own_pot,
-    parts_ref,
     field_0,
     field_1,
     field_2,
     mat_ref,
+    mixed,
     potential,
     stage,
     stage_pot,
     turned,
+    partial,
     rolled,
     packed,
     part,
@@ -105,6 +76,7 @@
     recv,
     send_pot,
     recv_pot,
+    pass_sem,
     halo_send,
     halo_recv,
     out_send,
@@ -118,14 +90,19 @@
     chips = n // 2
     slabs = n // 2
     total_planes = slabs * planes
-    first_worker = 2 * (chips // 2 - 1)
+    stride = chips // BANDS
     workers = 2 * BANDS
+
+    def worker(b, half):
+        return 2 * stride * b + half
+
     me = lax.axis_index("grid")
     kpt = lax.axis_index("kpt")
     core = lax.rem(me, 2)
     partner = me + 1 - 2 * core
-    is_worker = (me >= first_worker) & (me < first_worker + workers)
-    my_band = lax.div(me - first_worker, 2)
+    is_worker = lax.rem(lax.div(me, 2), stride) == 0
+    my_band = lax.div(lax.div(me, 2), stride)
+    my_place = 2 * my_band + core
     my_half = lax.div(me, slabs)
     my_slot = lax.rem(me, slabs)
 
@@ -133,13 +110,11 @@
         pltpu.make_async_copy(src, dst, load_sem.at[i])
         for i, (src, dst) in enumerate(
             (
-                (table_hbm, table_ref),
                 (kweight_hbm, kweight_ref),
                 (lowest_hbm, lowest_ref),
                 (cut_hbm, cut_ref),
                 (upper_hbm, upper_ref),
                 (fermi_hbm, fermi_ref),
-                (parts_hbm, parts_ref),
                 (pot_hbm, own_pot),
                 (bands_hbm.at[:, 0], own.at[0]),
                 (bands_hbm.at[:, 1], own.at[1]),
@@ -165,11 +140,10 @@
     @pl.when(jnp.logical_not(is_worker))
     def _():
         for w in range(workers):
-            greet(kpt, first_worker + w)
-
-    loads[7].wait()
-    loads[8].wait()
-    loads[9].wait()
+            greet(kpt, worker(w // 2, w % 2))
+
+    for load in loads[5:]:
+        load.wait()
     pl.semaphore_wait(
         barrier, jnp.where(is_worker, n - 1 + members_k - 1, workers + members_k - 1)
     )
@@ -186,18 +160,39 @@
 
     def deliver(i):
         b = 1 - my_half if i == 0 else my_half
-        target = first_worker + 2 * b + my_half
+        target = worker(b, my_half)
         wave = remote(own.at[b], stage.at[my_slot], send.at[i], recv.at[my_slot], target)
         pot = remote(own_pot, stage_pot.at[my_slot], send_pot.at[i], recv_pot.at[my_slot], target)
         return wave, pot, target
 
+    gives_pot = lax.rem(my_slot, members_k) == kpt
+    for i in range(BANDS):
+        wave, pot, target = deliver(i)
+
+        @pl.when((target != me) & gives_pot)
+        def _():
+            pot.start()
+
     for i in range(BANDS):
         wave, pot, target = deliver(i)
 
         @pl.when(target != me)
         def _():
             wave.start()
-            pot.start()
+
+    def pass_pot(slot, d):
+        return pltpu.make_async_remote_copy(
+            src_ref=stage_pot.at[slot],
+            dst_ref=stage_pot.at[slot],
+            send_sem=pass_sem.at[slot, d],
+            recv_sem=recv_pot.at[slot],
+            device_id=(lax.rem(kpt + d, members_k), me),
+            device_id_type=MESH,
+        )
+
+    def land_pot(slot):
+        here = stage_pot.at[slot]
+        remote(here, here, send_pot.at[0], recv_pot.at[slot], partner).wait_recv()
 
     lane = lax.broadcasted_iota(jnp.int32, (8, LANES), 1)
     row = lax.broadcasted_iota(jnp.int32, (8, LANES), 0)
@@ -213,8 +208,8 @@
     def spread(scalar):
         return jnp.full((8, LANES), scalar)
 
-    for i in range(7):
-        loads[i].wait()
+    for load in loads[:5]:
+        load.wait()
 
     low_end, cut_end, high_end = (spread(r[0]) for r in (lowest_ref, cut_ref, upper_ref))
     half_width = (high_end - cut_end) / 2.0
@@ -249,14 +244,24 @@
         scale = 2.0 / half_width
         weights = [scale * (-0.5 * c) for c in coefficients]
 
+        for r in range(LANES // 8):
+            target = row + 8 * r
+            target_z = jnp.where(target < SIDE, target, target - SIDE)
+            source_z = jnp.where(first, lane, lane - SIDE)
+            gap = target_z - source_z
+            apart = jnp.abs(gap)
+            near, wrap = zero, zero
+            for j in range(1, REACH + 1):
+                near = jnp.where(apart == j, weights[j], near)
+                wrap = jnp.where(apart == SIDE - j, weights[j], wrap)
+            across_sign = jnp.where((gap < 0) == (target < SIDE), sin_z, -sin_z)
+            same = (target < SIDE) == first
+            entry = jnp.where(same, near + cos_z * wrap, across_sign * wrap)
+            entry = jnp.where(used & (target < USED), entry, 0.0)
+            mixed[pl.ds(8 * r, 8), :] = entry
         for r in range(LANES // 16):
             rows = pl.ds(16 * r, 16)
-            cosine = jnp.concatenate([cos_z, cos_z], axis=0)
-            sine = jnp.concatenate([sin_z, sin_z], axis=0)
-            entry = (
-                parts_ref[0, rows, :] + cosine * parts_ref[1, rows, :] + sine * parts_ref[2, rows, :]
-            )
-            entry = entry * jnp.concatenate([scale, scale], axis=0)
+            entry = mixed[rows, :]
             high = entry.astype(jnp.bfloat16)
             rest = (entry - high.astype(jnp.float32)).astype(jnp.bfloat16)
             lower = pl.ds(LANES + 16 * r, 16)
@@ -321,17 +326,13 @@
                     potential[slot * planes + p, pl.ds(8 * t, 8), :] = v
 
         def take(i, carry):
-            slot = jnp.where(core == 0, slabs - 1 - i, i)
+            slot = jnp.where(my_band == 0, jnp.where(core == 0, i, slabs - 1 - i), jnp.where(core == 0, slabs - 1 - i, i))
 
             @pl.when(half_base + slot != me)
             def _():
                 remote(stage.at[slot], stage.at[slot], send.at[0], recv.at[slot], partner).wait_recv()
-                remote(
-                    stage_pot.at[slot], stage_pot.at[slot], send_pot.at[0], recv_pot.at[slot], partner
-                ).wait_recv()
 
             unpack(slot)
-            unpack_pot(slot)
             return carry
 
         half_base = core * slabs
@@ -341,10 +342,26 @@
             own_flat = own.reshape(BANDS, 2 * planes * CHUNKS, LANES)
             for r in range(2 * planes * CHUNKS // 8):
                 flat[my_slot, pl.ds(8 * r, 8), :] = own_flat[my_band, pl.ds(8 * r, 8), :]
-            for c in range(CHUNKS):
-                part_of = pl.ds(c * LANES, LANES)
-                stage_pot[my_slot, :, part_of] = own_pot[:, part_of]
-
+
+            @pl.when(gives_pot)
+            def _():
+                for c in range(CHUNKS):
+                    part_of = pl.ds(c * LANES, LANES)
+                    stage_pot[my_slot, :, part_of] = own_pot[:, part_of]
+
+        def spread_pot(slot, carry):
+            @pl.when(lax.rem(slot, members_k) == kpt)
+            def _():
+                @pl.when(half_base + slot != me)
+                def _():
+                    land_pot(slot)
+
+                for d in range(1, members_k):
+                    pass_pot(slot, d).start()
+
+            return carry
+
+        lax.fori_loop(0, slabs, spread_pot, 0)
         lax.fori_loop(0, slabs, take, 0)
 
         body = pl.ds(PAD, SIDE)
@@ -370,28 +387,76 @@
                     hold(side, p, t, field_0[base + p, pl.ds(PAD + 8 * t, 8), :])
             halo(field_0, side, 0).start()
 
-        def apply(f, k):
-            base = k * planes
-            middle = [f[base + planes + p, body, :] for p in range(planes)]
-            rows = jnp.concatenate(middle, axis=0)
+        def take_pot(i, carry):
+            slot = lax.rem(kpt + i, slabs)
+
+            @pl.when(lax.rem(slot, members_k) != kpt)
+            def _():
+                land_pot(slot)
+
+            unpack_pot(slot)
+            return carry
+
+        lax.fori_loop(0, slabs, take_pot, 0)
+
+        def third_of(f, spans):
+            rows = jnp.concatenate(
+                [f[planes + q, body, :] for start in spans for q in qs(start)], axis=0
+            )
             high = rows.astype(jnp.bfloat16)
             rest = (rows - high.astype(jnp.float32)).astype(jnp.bfloat16)
             both = jnp.concatenate([high, rest], axis=1)
             third = jnp.dot(both, mat_ref[...], preferred_element_type=jnp.float32)
-            third = third[:, :LANES] + third[:, LANES:]
+            return third[:, :LANES] + third[:, LANES:]
+
+        def qs(start):
+            return [start + p for p in range(planes)]
+
+        def apply(f, spans, sides):
+            third = third_of(f, spans)
+            for i, start in enumerate(spans):
+                side = sides[i]
+                for t in range(TILES):
+                    tile = pl.ds(PAD + 8 * t, 8)
+                    low = planes if side == 0 else 0
+                    high = 2 * planes if side == 1 else 3 * planes
+                    window = [
+                        f[start + q, tile, :] if low <= q < high else None
+                        for q in range(3 * planes)
+                    ]
+                    for p in range(planes):
+                        value = window[planes + p]
+                        at = (i * planes + p) * SIDE + 8 * t
+                        total = third[at : at + 8, :]
+                        total = total + value * potential[start + p, pl.ds(8 * t, 8), :]
+                        for j in range(1, REACH + 1):
+                            above = f[planes + start + p, pl.ds(PAD + 8 * t + j, 8), :]
+                            below = f[planes + start + p, pl.ds(PAD + 8 * t - j, 8), :]
+                            around = above + below
+                            for q in (planes + p + j, planes + p - j):
+                                if window[q] is not None:
+                                    around = around + window[q]
+                            total = total + weights[j] * around
+                        yield i, p, start + p, t, tile, value, total
+
+        def finish(f, start, side):
             for t in range(TILES):
                 tile = pl.ds(PAD + 8 * t, 8)
-                window = [f[base + i, tile, :] for i in range(3 * planes)]
+                there = total_planes + planes if side == 1 else 0
+                window = [f[there + q, tile, :] for q in range(planes)]
                 for p in range(planes):
-                    value = window[planes + p]
-                    total = third[p * SIDE + 8 * t : p * SIDE + 8 * t + 8, :]
-                    total = total + value * potential[base + p, pl.ds(8 * t, 8), :]
+                    total = partial[side * planes + p, pl.ds(8 * t, 8), :]
                     for j in range(1, REACH + 1):
-                        around = window[planes + p + j] + window[planes + p - j]
-                        above = f[base + planes + p, pl.ds(PAD + 8 * t + j, 8), :]
-                        below = f[base + planes + p, pl.ds(PAD + 8 * t - j, 8), :]
-                        total = total + weights[j] * (around + (above + below))
-                    yield p, base + planes + p, t, tile, value, total
+                        q = p + j - planes if side == 1 else planes + p - j
+                        if 0 <= q < planes:
+                            total = total + weights[j] * window[q]
+                    yield p, start + p, t, tile, total
+
+        outer = (0, total_planes - planes)
+
+        def begin(f):
+            for i, p, _, t, _, _, total in apply(f, outer, (0, 1)):
+                partial[i * planes + p, pl.ds(8 * t, 8), :] = total
 
         def await_halos(f, parity):
             for side in range(2):
@@ -407,24 +472,27 @@
             now, then, before = (fields[(c + i) % 3] for i in range(3))
             gain = jnp.where(m == 1, 0.5, 1.0)
 
-            def block(k, side=None):
-                for p, plane, t, tile, _, total in apply(now, k):
-                    following = gain * total - before[plane, tile, :]
-                    put(then, plane, t, following)
-                    if side is not None:
-                        hold(side, p, t, following)
+            def settle(plane, t, tile, total):
+                following = gain * total - before[planes + plane, tile, :]
+                put(then, planes + plane, t, following)
+                return following
+
+            begin(now)
 
             def inner(k, carry):
-                block(k)
+                start = planes + 2 * planes * k
+                spans = (start, start + planes)
+                for _, _, plane, t, tile, _, total in apply(now, spans, (None, None)):
+                    settle(plane, t, tile, total)
                 return carry
 
-            lax.fori_loop(1, slabs - 1, inner, 0)
+            lax.fori_loop(0, slabs // 2 - 1, inner, 0)
             parity = lax.rem(m - 1, 2)
             await_halos(now, parity)
-            block(0, 0)
-            halo(then, 0, 1 - parity).start()
-            block(slabs - 1, 1)
-            halo(then, 1, 1 - parity).start()
+            for side in range(2):
+                for p, plane, t, tile, total in finish(now, outer[side], side):
+                    hold(side, p, t, settle(plane, t, tile, total))
+                halo(then, side, 1 - parity).start()
 
         def three(r, carry):
             for c in range(3):
@@ -496,36 +564,47 @@
 
         lax.fori_loop(0, slabs, pack, 0)
 
-        def sums(k, carry):
-            tops, bottoms = list(carry[0]), list(carry[1])
-            for _, _, t, _, value, total in apply(final, k):
-                tops[t % 2] = tops[t % 2] + value * total
-                bottoms[t % 2] = bottoms[t % 2] + value * value
-            return tuple(tops), tuple(bottoms)
+        begin(final)
+
+        def gather_up(sums, t, value, total):
+            tops, bottoms = sums
+            tops[t % 2] = tops[t % 2] + value * total
+            bottoms[t % 2] = bottoms[t % 2] + value * value
+
+        def inner_sums(k, carry):
+            sums = list(carry[0]), list(carry[1])
+            start = planes + 2 * planes * k
+            for _, _, _, t, _, value, total in apply(
+                final, (start, start + planes), (None, None)
+            ):
+                gather_up(sums, t, value, total)
+            return tuple(sums[0]), tuple(sums[1])
 
         carry = ((zero, zero), (zero, zero))
-        carry = lax.fori_loop(1, slabs - 1, sums, carry)
+        carry = lax.fori_loop(0, slabs // 2 - 1, inner_sums, carry)
+        tops, bottoms = sums = list(carry[0]), list(carry[1])
         await_halos(final, DEGREE % 2)
-        carry = sums(0, carry)
-        tops, bottoms = sums(slabs - 1, carry)
+        for side in range(2):
+            for _, plane, t, tile, total in finish(final, outer[side], side):
+                gather_up(sums, t, final[planes + plane, tile, :], total)
         top = jnp.sum(tops[0] + tops[1], keepdims=True)
         bottom = jnp.sum(bottoms[0] + bottoms[1], keepdims=True)
         left = lax.broadcasted_iota(jnp.int32, (1, LANES), 1) < LANES // 2
-        part[me - first_worker] = jnp.where(left, top, bottom)
+        part[my_place] = jnp.where(left, top, bottom)
         for d in range(1, n):
             remote(
-                part.at[me - first_worker],
-                part.at[me - first_worker],
+                part.at[my_place],
+                part.at[my_place],
                 send_red.at[d],
-                recv_red.at[me - first_worker],
+                recv_red.at[my_place],
                 lax.rem(me + d, n),
             ).start()
 
     for w in range(workers):
 
-        @pl.when(me != first_worker + w)
+        @pl.when(me != worker(w // 2, w % 2))
         def _():
-            remote(part.at[w], part.at[w], send_red.at[0], recv_red.at[w], first_worker + w).wait_recv()
+            remote(part.at[w], part.at[w], send_red.at[0], recv_red.at[w], partner).wait_recv()
 
     kweight, fermi = kweight_ref[0], fermi_ref[0]
     e_half, c_half = half_width[0:1, :], centre[0:1, :]
@@ -567,6 +646,9 @@
         @pl.when(target != me)
         def _():
             wave.wait_send()
+
+        @pl.when((target != me) & gives_pot)
+        def _():
             pot.wait_send()
 
     for d in range(1, members_k):
@@ -576,10 +658,10 @@
     def _():
         for d in range(1, n):
             remote(
-                part.at[me - first_worker],
-                part.at[me - first_worker],
+                part.at[my_place],
+                part.at[my_place],
                 send_red.at[d],
-                recv_red.at[me - first_worker],
+                recv_red.at[my_place],
                 lax.rem(me + d, n),
             ).wait_send()
 
@@ -598,12 +680,21 @@
 
         lax.fori_loop(0, slabs, drain, 0)
 
+        def drain_pot(slot, carry):
+            @pl.when(lax.rem(slot, members_k) == kpt)
+            def _():
+                for d in range(1, members_k):
+                    pass_pot(slot, d).wait_send()
+
+            return carry
+
+        lax.fori_loop(0, slabs, drain_pot, 0)
+
 
 def per_device(bands, potential, table, kweight, lowest, cut, upper, fermi):
     n = lax.axis_size("grid")
     members_k = lax.axis_size("kpt")
     planes = bands.shape[3]
-    parts = jnp.asarray(np.stack(third_parts()))
     pieces = 2 * planes
     flat = pieces * CHUNKS
 
@@ -628,10 +719,9 @@
             jax.ShapeDtypeStruct((1, BANDS), f32),
             jax.ShapeDtypeStruct((1, 1), f32),
         ),
-        in_specs=[anywhere] * 6 + [hbm] * 3,
+        in_specs=[scalar] + [hbm] * 7,
         out_specs=(hbm, scalar, scalar),
         scratch_shapes=[
-            smem((1, 3), jnp.int32),
             smem((1,), f32),
             smem((1,), f32),
             smem((1,), f32),
@@ -639,24 +729,26 @@
             smem((1,), f32),
             vmem((BANDS, flat, 1, LANES), f32),
             vmem((planes, SIDE * SIDE), f32),
-            vmem((3, LANES, LANES), f32),
             vmem((total_planes + 2 * planes, ROWS, LANES), f32),
             vmem((total_planes + 2 * planes, ROWS, LANES), f32),
             vmem((total_planes + 2 * planes, ROWS, LANES), f32),
             vmem((2 * LANES, 2 * LANES), jnp.bfloat16),
+            vmem((LANES, LANES), f32),
             vmem((total_planes, SIDE, LANES), f32),
             vmem((slabs, flat, 1, LANES), f32),
             vmem((slabs, planes, SIDE * SIDE), f32),
             vmem((2, planes, SIDE, LANES), f32),
             vmem((2 * planes, SIDE, LANES), f32),
+            vmem((2 * planes, SIDE, LANES), f32),
             vmem((slabs, flat, 1, LANES), f32),
             vmem((workers, 1, LANES), f32),
             vmem((members_k, 1, LANES), f32),
-            dma((10,)),
+            dma((8,)),
             dma((BANDS,)),
             dma((slabs,)),
             dma((BANDS,)),
             dma((slabs,)),
+            dma((slabs, members_k)),
             dma((2,)),
             dma((2, 2)),
             dma((slabs,)),
@@ -667,9 +759,9 @@
             dma((members_k,)),
         ],
         compiler_params=pltpu.CompilerParams(
-            collective_id=0, has_side_effects=True, vmem_limit_bytes=48 * 1024 * 1024
+            collective_id=0, has_side_effects=True, vmem_limit_bytes=62 * 1024 * 1024
         ),
-    )(table, kweight, lowest, cut, upper, fermi, raw, potential, parts)
+    )(table, kweight, lowest, cut, upper, fermi, raw, potential)
     filtered = out.reshape(pieces, CHUNKS, BANDS, LANES).transpose(0, 2, 1, 3)
     filtered = filtered.reshape(2, planes, BANDS, SIDE * SIDE).transpose(0, 2, 1, 3)[None]
     return filtered, energy, total[0]

time: 53.5 us -> 47.7 us (0.89)
  the two profiles are of different devices: /device:TPU:0 before, /device:TPU:16 now
where the time goes in v2:
time: 47.7 us; the launch traced here: 47.5 us
  Pallas kernels  39.7 us (83%)
  between operations  5.64 us (12%)
  local copies, waits for them, and re-layouts  2.15 us (5%)
    pallas_call x1, Pallas kernels, per_device(): pl.pallas_call(functools.partial(kernel, n, members_k, planes), name='che...  39.7 us
    unnamed x4, local copies, waits for them, and re-layouts  2.15 us

profile of v2, /device:TPU:16, one launch (start us, length us, event | category | flops | bytes accessed | tf_op | source)
XLA Modules:
  0.0 47.5 jit_solution(11731858633656266817)
XLA Ops:
  3.9 39.7 %cheb.1 = (f32[216,2,1,128]{3,2,1,0:T(1,128)}, f32[1,2]{1,0:T(1,128)}, f32[1,1]{1,0:T(1,128)}) custom-call(s32[1,3]{1,0:T(1,128)} %table_ref.1, f32[1]{0:T(128)S(6)} %copy.14.kweight_hbm, f32[1]{0:T(128)S(6)} %copy.15.lowest_hbm, f32[1]{0:T(128)S(6)} %copy.16.cut_hbm, f32[1]{0:T(128)S(6)} %copy.17.upper_hbm, f32[1]{0:T(128)S(6)} %copy.18.fermi_hbm, ...), custom_call_target="tpu_custom_call" | custom-call | tf_op jit(solution)/shard_map/cheb/pallas_call | solution.py:714
  43.6 0.0 copy-start
  43.6 1.6 %copy.19 = f32[1,2,2,6,2304]{4,2,3,1,0:T(2,128)} copy(f32[1,2,2,6,2304]{4,2,3,1,0:T(2,128)} %bitcast.19) | data formatting | bytes 442368
  45.2 0.0 copy-done
  45.2 0.5 %copy.20 = f32[1,2]{1,0:T(1,128)} copy(f32[1,2]{1,0:T(1,128)S(1)} %copy-done) | data formatting | bytes 16
Async XLA Ops:
  43.6 1.7 %copy-start = (f32[1,2]{1,0:T(1,128)S(1)}, f32[1,2]{1,0:T(1,128)}, u32[]{:S(2)}) copy-start(f32[1,2]{1,0:T(1,128)} %get-tuple-element.13) | copy-start | bytes 28

commit v3 on v2

--- a/solution.py
+++ b/solution.py
@@ -71,6 +71,8 @@
     packed,
     part,
     part_k,
+    relay_in,
+    relay_out,
     load_sem,
     send,
     recv,
@@ -85,6 +87,8 @@
     recv_red,
     send_k,
     recv_k,
+    relay_send,
+    relay_recv,
 ):
     fields = (field_0, field_1, field_2)
     chips = n // 2
@@ -103,6 +107,8 @@
     is_worker = lax.rem(lax.div(me, 2), stride) == 0
     my_band = lax.div(lax.div(me, 2), stride)
     my_place = 2 * my_band + core
+    relay_on = chips == 2 * BANDS
+    relayed = is_worker & (core == 1) if relay_on else jnp.bool_(False)
     my_half = lax.div(me, slabs)
     my_slot = lax.rem(me, slabs)
 
@@ -175,10 +181,19 @@
 
     for i in range(BANDS):
         wave, pot, target = deliver(i)
-
-        @pl.when(target != me)
+        around = relayed if i == 0 else False
+
+        @pl.when((target != me) & jnp.logical_not(around))
         def _():
             wave.start()
+
+        if relay_on and i == 0:
+
+            @pl.when(relayed)
+            def _():
+                remote(
+                    own.at[1 - my_half], relay_in, send.at[0], relay_recv.at[0], lax.rem(me + n - 2, n)
+                ).start()
 
     def pass_pot(slot, d):
         return pltpu.make_async_remote_copy(
@@ -193,6 +208,26 @@
     def land_pot(slot):
         here = stage_pot.at[slot]
         remote(here, here, send_pot.at[0], recv_pot.at[slot], partner).wait_recv()
+
+    if relay_on:
+
+        @pl.when(jnp.logical_not(is_worker) & (core == 1))
+        def _():
+            source, sink = lax.rem(me + 2, n), lax.rem(me + n - 2, n)
+            half, slot = lax.div(source, slabs), lax.rem(source, slabs)
+            band = lax.div(lax.div(source, 2), stride)
+            remote(relay_in, relay_in, relay_send.at[0], relay_recv.at[0], partner).wait_recv()
+            onward = remote(
+                relay_in, stage.at[slot], relay_send.at[0], recv.at[slot], worker(1 - half, half)
+            )
+            onward.start()
+            remote(relay_out, relay_out, relay_send.at[1], relay_recv.at[1], partner).wait_recv()
+            homeward = remote(
+                relay_out, out_ref.at[:, band], relay_send.at[1], out_recv.at[band], sink
+            )
+            homeward.start()
+            onward.wait_send()
+            homeward.wait_send()
 
     lane = lax.broadcasted_iota(jnp.int32, (8, LANES), 1)
     row = lax.broadcasted_iota(jnp.int32, (8, LANES), 0)
@@ -521,7 +556,7 @@
             )
 
         def pack(i, carry):
-            slot = jnp.where(core == 0, i, slabs - 1 - i)
+            slot = jnp.where(core == my_band, slabs - 1 - i, i + 1 - 2 * lax.rem(i, 2))
 
             for p in range(planes):
                 plane = planes + slot * planes + p
@@ -552,9 +587,24 @@
                     for j in range(PER_TILE):
                         flat_packed[slot, pl.ds(base + j, TILES, stride=PER_TILE), :] = rows[j]
 
-            @pl.when(core * slabs + slot != me)
+            goal = core * slabs + slot
+            aside = goal == lax.rem(me - core + 5, n) if relay_on else jnp.bool_(False)
+
+            @pl.when((goal != me) & jnp.logical_not(aside))
             def _():
                 give(slot).start()
+
+            if relay_on:
+
+                @pl.when(aside)
+                def _():
+                    remote(
+                        packed.at[slot],
+                        relay_out,
+                        out_send.at[slot],
+                        relay_recv.at[1],
+                        lax.rem(me - core + n - 1, n),
+                    ).start()
 
             @pl.when(core * slabs + slot == me)
             def _():
@@ -743,6 +793,8 @@
             vmem((slabs, flat, 1, LANES), f32),
             vmem((workers, 1, LANES), f32),
             vmem((members_k, 1, LANES), f32),
+            vmem((flat, 1, LANES), f32),
+            vmem((flat, 1, LANES), f32),
             dma((8,)),
             dma((BANDS,)),
             dma((slabs,)),
@@ -757,6 +809,8 @@
             dma((workers,)),
             dma((members_k,)),
             dma((members_k,)),
+            dma((2,)),
+            dma((2,)),
         ],
         compiler_params=pltpu.CompilerParams(
             collective_id=0, has_side_effects=True, vmem_limit_bytes=62 * 1024 * 1024

time: 47.7 us -> 46.2 us (0.969)
  the two profiles are of different devices: /device:TPU:16 before, /device:TPU:0 now
where the time goes in v3:
time: 46.2 us; the launch traced here: 45.9 us
  Pallas kernels  38.2 us (83%)
  between operations  5.64 us (12%)
  local copies, waits for them, and re-layouts  2.15 us (5%)
    pallas_call x1, Pallas kernels, per_device(): pl.pallas_call(functools.partial(kernel, n, members_k, planes), name='che...  38.2 us
    unnamed x4, local copies, waits for them, and re-layouts  2.15 us

profile of v3, /device:TPU:0, one launch (start us, length us, event | category | flops | bytes accessed | tf_op | source)
XLA Modules:
  0.0 45.9 jit_solution(4360504257681486929)
XLA Ops:
  3.9 38.2 %cheb.1 = (f32[216,2,1,128]{3,2,1,0:T(1,128)}, f32[1,2]{1,0:T(1,128)}, f32[1,1]{1,0:T(1,128)}) custom-call(s32[1,3]{1,0:T(1,128)} %table_ref.1, f32[1]{0:T(128)S(6)} %copy.14.kweight_hbm, f32[1]{0:T(128)S(6)} %copy.15.lowest_hbm, f32[1]{0:T(128)S(6)} %copy.16.cut_hbm, f32[1]{0:T(128)S(6)} %copy.17.upper_hbm, f32[1]{0:T(128)S(6)} %copy.18.fermi_hbm, ...), custom_call_target="tpu_custom_call" | custom-call | tf_op jit(solution)/shard_map/cheb/pallas_call | solution.py:764
  42.0 0.0 copy-start
  42.0 1.6 %copy.19 = f32[1,2,2,6,2304]{4,2,3,1,0:T(2,128)} copy(f32[1,2,2,6,2304]{4,2,3,1,0:T(2,128)} %bitcast.19) | data formatting | bytes 442368
  43.7 0.0 copy-done
  43.7 0.5 %copy.20 = f32[1,2]{1,0:T(1,128)} copy(f32[1,2]{1,0:T(1,128)S(1)} %copy-done) | data formatting | bytes 16
Async XLA Ops:
  42.0 1.7 %copy-start = (f32[1,2]{1,0:T(1,128)S(1)}, f32[1,2]{1,0:T(1,128)}, u32[]{:S(2)}) copy-start(f32[1,2]{1,0:T(1,128)} %get-tuple-element.13) | copy-start | bytes 28
